TPU v7x, 32 devices: a whole 2x2x4 slice. The times are simulated.
32 devices in a mesh: scene: 2 (over y), tile: 4 (over z), half: 2 (over x), band: 2 (over core).
Axes of the slice: x: 2, y: 2, z: 4, core: 2. Of those that a mesh axis runs over, the one named last changes fastest.
Arguments:
- optical: bfloat16 [16, 2, 512, 512], P(('scene', 'tile'), 'band', 'half'), parts along dimension 0, may hold values from -64 to 64
- sar: bfloat16 [2, 8192, 512], P('band', ('scene', 'tile', 'half')), parts along dimension 1, may hold values from -64 to 64
- destination: int32 [128], P('scene'), parts along dimension 0, may hold values from 0 to 63, as said below
- peaks: int32 [16, 2, 8], P(('scene', 'tile', 'band')), parts along dimension 0, may hold values from 0 to 511
Outputs:
- surface: float32 [16, 512, 512], P(('scene', 'tile', 'band'), 'half'), parts along dimension 0
- peak_values: float32 [16, 8], P(('scene', 'tile', 'band')), parts along dimension 0
There are 2 independent parts, one for each index of `scene`. A program takes and returns all parts, laid end to end along the dimension named above; each array names one. Nothing has to cross between parts.
Inputs may be any that keep to these rules, and one draw needn't show every extreme that they name: destination holds every block position 0 to 63 once; the 8 blocks that start at each multiple of 8 are sent one into each run of 8 positions that starts at a multiple of 8.
All inputs are finite; a program needn't handle non-finite values.
Results may differ from a plain program's by a relative error of at most 0.014.
Values may be sent and summed in bfloat16 or wider, within the bound.
A program may use at most 64 MiB of HBM per device.

v0:
```python
import functools
import math

import jax
import jax.numpy as jnp
import numpy as np
from jax import lax
from jax.experimental import pallas as pl
from jax.experimental.pallas import tpu as pltpu
from jax.sharding import PartitionSpec as P

MESH = pl.DeviceIdType.MESH

precise = lax.Precision.HIGHEST
EPSILON = 1e-06


def fourier_tables(extent):
    places = jnp.arange(extent, dtype=jnp.int32)
    phases = places[:, None] * places[None, :] % extent
    angles = phases.astype(jnp.float32) * (2.0 * math.pi / extent)
    return (jnp.cos(angles), jnp.sin(angles))


def fourier_pair(table):
    upper = table.astype(jnp.bfloat16)
    lower = (table - upper.astype(jnp.float32)).astype(jnp.bfloat16)
    return (upper, lower)


def column_spectrum(samples, table_upper, table_lower):
    extent = samples.shape[-1]
    values = samples.reshape(-1, extent)
    spectrum = jnp.dot(values, table_upper, preferred_element_type=jnp.float32) + jnp.dot(
        values, table_lower, preferred_element_type=jnp.float32
    )
    return spectrum.astype(jnp.bfloat16).reshape(samples.shape[:-1] + (2 * extent,))


def row_spectrum(columns, table_upper, table_lower):
    line_count = columns.shape[-3]
    stacked = jnp.concatenate([columns[..., 0, :], columns[..., 1, :]], axis=-2)
    result = jnp.einsum("kr,...rc->...kc", table_upper, stacked, preferred_element_type=jnp.float32)
    result = result + jnp.einsum(
        "kr,...rc->...kc", table_lower, stacked, preferred_element_type=jnp.float32
    )
    return (result[..., :line_count, :], result[..., line_count:, :])


def relay_blocks(parcel):
    layout = parcel.shape
    merged = parcel.reshape(layout[:1] + (layout[1] * layout[2],) + layout[3:])
    arrived = lax.all_to_all(merged, ("tile", "half"), split_axis=1, concat_axis=1, tiled=True)
    return arrived.reshape(layout)


def generic(optical, sar, destination, peaks):
    tile_count = lax.axis_size("tile")
    half_count = lax.axis_size("half")
    band_count = lax.axis_size("band")
    group_size = tile_count * half_count
    patch_dev, local_bands, quarter, extent = optical.shape
    col_width = extent // half_count
    block_lines = sar.shape[1] // group_size
    band_total = local_bands * band_count
    pixel_count = extent * extent
    patch_total = patch_dev * tile_count
    kept_patches = patch_dev // band_count
    cosine_table, sine_table = fourier_tables(extent)
    col_upper, col_lower = fourier_pair(jnp.concatenate([cosine_table, -sine_table], axis=1))
    row_full = jnp.concatenate(
        [
            jnp.concatenate([cosine_table, sine_table], axis=1),
            jnp.concatenate([-sine_table, cosine_table], axis=1),
        ],
        axis=0,
    )
    row_upper, row_lower = fourier_pair(row_full)
    tile_at = lax.axis_index("tile")
    half_at = lax.axis_index("half")
    band_at = lax.axis_index("band")
    device_at = lax.axis_index(("tile", "half"))
    own_blocks = lax.dynamic_slice_in_dim(destination, device_at * group_size, group_size)
    send_order = jnp.argsort(own_blocks // group_size)
    inverse = (
        jnp.zeros_like(destination)
        .at[destination]
        .set(jnp.arange(destination.shape[0], dtype=jnp.int32))
    )
    opt_values = optical.astype(jnp.float32)
    opt_sums = jnp.sum(opt_values, axis=(2, 3))
    opt_squares = jnp.sum(opt_values * opt_values, axis=(2, 3))
    sar_values = sar.astype(jnp.float32).reshape(local_bands, group_size, block_lines * extent)
    sar_sums = jnp.sum(sar_values, axis=2)
    sar_squares = jnp.sum(sar_values * sar_values, axis=2)
    map_device = own_blocks // group_size
    map_patch = (
        map_device // half_count * patch_dev + own_blocks % group_size * block_lines // quarter
    )
    member = (map_patch[:, None] == jnp.arange(patch_total, dtype=jnp.int32)[None, :]).astype(
        jnp.float32
    )
    sar_stats = jnp.dot(
        jnp.stack([sar_sums, sar_squares]).reshape(2 * local_bands, group_size),
        member,
        precision=precise,
        preferred_element_type=jnp.float32,
    )
    statistics = jnp.zeros((2, 2, band_total, patch_total), jnp.float32)
    opt_part = jnp.transpose(jnp.stack([opt_sums, opt_squares]), (0, 2, 1))
    statistics = lax.dynamic_update_slice(
        statistics, opt_part[None], (0, 0, band_at * local_bands, tile_at * patch_dev)
    )
    statistics = lax.dynamic_update_slice(
        statistics,
        sar_stats.reshape(2, local_bands, patch_total)[None],
        (1, 0, band_at * local_bands, 0),
    )
    totals = lax.psum(statistics, ("tile", "half", "band"))
    centered = totals[:, 1] - totals[:, 0] * totals[:, 0] / pixel_count
    energy = jnp.sum(centered, axis=1) / (band_total * pixel_count)
    norm_scale = lax.rsqrt(band_total * pixel_count * (energy[0] + EPSILON) * (energy[1] + EPSILON))
    first_patch = tile_at * patch_dev + band_at * kept_patches
    norm_mine = lax.dynamic_slice_in_dim(norm_scale, first_patch, kept_patches)
    slant_spectra = column_spectrum(sar, col_upper, col_lower).reshape(
        local_bands, group_size, block_lines, 2, half_count, col_width
    )
    outgoing = jnp.take(slant_spectra, send_order, axis=1).reshape(
        local_bands, tile_count, half_count, block_lines, 2, half_count, col_width
    )
    outgoing = jnp.transpose(outgoing, (0, 1, 5, 2, 3, 4, 6))
    arrived = relay_blocks(outgoing).reshape(
        local_bands, group_size * half_count, block_lines, 2, col_width
    )
    sources = lax.dynamic_slice_in_dim(
        inverse, tile_at * half_count * group_size, half_count * group_size
    )
    slot_index = (
        sources // group_size * half_count
        + jnp.arange(half_count * group_size, dtype=jnp.int32) // group_size
    )
    placed = jnp.take(arrived, slot_index, axis=1).reshape(
        local_bands, half_count, patch_dev, quarter, 2, col_width
    )
    placed = jnp.transpose(placed, (2, 0, 1, 3, 4, 5)).reshape(
        patch_dev, local_bands, extent, 2, col_width
    )
    sar_real, sar_imag = row_spectrum(placed, row_upper, row_lower)
    spectra = column_spectrum(optical, col_upper, col_lower).reshape(
        patch_dev, local_bands, quarter, 2, half_count, col_width
    )
    real_part, imag_part = row_spectrum(
        jnp.squeeze(
            lax.all_to_all(spectra, "half", split_axis=4, concat_axis=2, tiled=True), axis=4
        ),
        row_upper,
        row_lower,
    )
    opt_real = real_part
    opt_imag = imag_part
    rows_at = jnp.arange(extent, dtype=jnp.int32)[:, None]
    cols_at = half_at * col_width + jnp.arange(col_width, dtype=jnp.int32)[None, :]
    keep_mask = jnp.where((rows_at == 0) & (cols_at == 0), 0.0, 1.0).astype(jnp.float32)
    opt_real = opt_real * keep_mask
    opt_imag = opt_imag * keep_mask
    sar_real = sar_real * keep_mask
    sar_imag = sar_imag * keep_mask
    cross_real = jnp.sum(opt_real * sar_real + opt_imag * sar_imag, axis=1)
    cross_imag = jnp.sum(opt_real * sar_imag - opt_imag * sar_real, axis=1)
    cross_term = jnp.stack([cross_real, cross_imag], axis=1)
    cross_sum = lax.psum_scatter(cross_term, "band", scatter_dimension=0, tiled=True)
    lag_real = (
        jnp.einsum("uk,pkc->puc", cosine_table, cross_sum[:, 0], precision=precise)
        - jnp.einsum("uk,pkc->puc", sine_table, cross_sum[:, 1], precision=precise)
    ) / extent
    lag_imag = (
        jnp.einsum("uk,pkc->puc", cosine_table, cross_sum[:, 1], precision=precise)
        + jnp.einsum("uk,pkc->puc", sine_table, cross_sum[:, 0], precision=precise)
    ) / extent
    lagged = jnp.stack([lag_real, lag_imag], axis=2).reshape(
        kept_patches, half_count, quarter, 2, col_width
    )
    pieces = lax.all_to_all(lagged, "half", split_axis=1, concat_axis=4, tiled=True)
    real_in = pieces[:, 0, :, 0, :]
    imag_in = pieces[:, 0, :, 1, :]
    correlation = (
        jnp.einsum("puc,cv->puv", real_in, cosine_table, precision=precise)
        - jnp.einsum("puc,cv->puv", imag_in, sine_table, precision=precise)
    ) / extent
    surface = correlation * norm_mine[:, None, None]
    local_rows = peaks[:, 0, :] - half_at * quarter
    row_hit = (
        local_rows[:, :, None] == jnp.arange(quarter, dtype=jnp.int32)[None, None, :]
    ).astype(jnp.float32)
    picked = jnp.einsum("pkr,prc->pkc", row_hit, surface, precision=precise)
    col_hit = (peaks[:, 1, :, None] == jnp.arange(extent, dtype=jnp.int32)[None, None, :]).astype(
        jnp.float32
    )
    local_values = jnp.sum(picked * col_hit, axis=2)
    peak_values = lax.psum(local_values, "half")
    return (surface, peak_values)


def half_tables(extent, half_count, chunk):
    width = extent // 2 // half_count
    places = np.arange(extent)
    phases = (places[:, None] * places[None, :]) % extent
    cosine = np.cos(phases * (2.0 * np.pi / extent))
    sine = np.sin(phases * (2.0 * np.pi / extent))
    forward, backward = [], []
    for half in range(half_count):
        span = slice(half * width, (half + 1) * width)
        real, imag = cosine[:, span].copy(), -sine[:, span]
        real_back, imag_back = 2.0 * cosine[span], -2.0 * sine[span]
        if half == 0:
            imag[:, 0] = cosine[:, extent // 2]
            real_back[0] = 1.0
            imag_back[0] = cosine[extent // 2]
        forward.append(np.concatenate([real, imag], axis=1))
        backward.append(np.concatenate([real_back, imag_back], axis=0))
    col_table = np.concatenate(forward, axis=1)
    lag_table = np.stack(backward)
    row_table = np.concatenate(
        [cosine.reshape(-1, chunk, extent), sine.reshape(-1, chunk, extent)], axis=1
    )
    return tuple(t.astype(jnp.bfloat16) for t in (col_table, row_table, lag_table))


def kernel(
    sizes,
    dest_ref,
    peaks_ref,
    sar_hbm,
    opt_hbm,
    col_hbm,
    row_hbm,
    lag_hbm,
    surface_ref,
    peak_ref,
    sar_v,
    opt_v,
    col_v,
    row_v,
    lag_v,
    sar_send,
    arrived,
    opt_send,
    opt_cols,
    sar_cols,
    sar_rows,
    cross_send,
    cross_recv,
    cross_own,
    cross_all,
    stat_send,
    stat_recv,
    last_send,
    last_recv,
    lags,
    lag_recv,
    load_sem,
    sar_ssem,
    sar_rsem,
    opt_ssem,
    opt_rsem,
    pair_ssem,
    pair_rsem,
):
    tiles, halves, bands, patch_dev, quarter, extent, lines, chunk, peak_count = sizes
    group = tiles * halves
    width = extent // 2 // halves
    chunks = extent // chunk
    per_half = chunks // halves
    tile, half, band = lax.axis_index("tile"), lax.axis_index("half"), lax.axis_index("band")
    me = tile * halves + half
    other_half = 1 - half
    other_band = 1 - band

    loads = [
        pltpu.make_async_copy(a, b, load_sem.at[i])
        for i, (a, b) in enumerate(
            [(sar_hbm, sar_v), (col_hbm, col_v), (opt_hbm, opt_v), (row_hbm, row_v), (lag_hbm, lag_v)]
        )
    ]
    for load in loads:
        load.start()

    barrier = pltpu.get_barrier_semaphore()
    for step in range(tiles):
        for shift in range(halves):
            if step or shift:
                pl.semaphore_signal(
                    barrier,
                    inc=1,
                    device_id={
                        "tile": lax.rem(tile + step, tiles),
                        "half": lax.rem(half + shift, halves),
                    },
                    device_id_type=MESH,
                )
    pl.semaphore_signal(barrier, inc=1, device_id={"band": other_band}, device_id_type=MESH)

    own_runs = [lax.div(dest_ref[me * group + j], group) for j in range(group)]

    def block_for(run):
        found = jnp.int32(0)
        for j in range(group):
            found = jnp.where(own_runs[j] == run, j, found)
        return found

    loads[0].wait()
    loads[1].wait()
    pl.semaphore_wait(barrier, group)

    def sar_copy(step, shift):
        to_half = lax.rem(half + shift, halves)
        return pltpu.make_async_remote_copy(
            src_ref=sar_send.at[step, to_half],
            dst_ref=arrived.at[me],
            send_sem=sar_ssem.at[step * halves + shift],
            recv_sem=sar_rsem.at[me],
            device_id={"tile": lax.rem(tile + step, tiles), "half": to_half},
            device_id_type=MESH,
        )

    copies = []
    order = sorted(range(tiles), key=lambda s: -min(s, tiles - s))
    for step in order:
        to_tile = lax.rem(tile + step, tiles)
        samples = jnp.concatenate(
            [sar_v[block_for(to_tile * halves + run)] for run in range(halves)], axis=0
        )
        spectra = jnp.dot(samples, col_v[...], preferred_element_type=jnp.float32)
        spectra = spectra.astype(jnp.bfloat16)
        for to_half in range(halves):
            piece = spectra[:, to_half * 2 * width : (to_half + 1) * 2 * width]
            sar_send[step, to_half] = piece.reshape(halves, lines, 2 * width)
        for shift in reversed(range(halves)):
            if step or shift:
                copy = sar_copy(step, shift)
                copy.start()
                copies.append(copy)
    arrived[me] = sar_send[0, half]

    opt_copies = []
    loads[2].wait()
    for turn, patch in enumerate((other_band, band)):
        spectra = jnp.dot(opt_v[patch], col_v[...], preferred_element_type=jnp.float32)
        spectra = spectra.astype(jnp.bfloat16)
        for to_half in range(halves):
            opt_send[turn, to_half] = spectra[:, to_half * 2 * width : (to_half + 1) * 2 * width]
        rows = pl.ds(pl.multiple_of(half * quarter, quarter), quarter)
        copy = pltpu.make_async_remote_copy(
            src_ref=opt_send.at[turn, other_half],
            dst_ref=opt_cols.at[turn, rows],
            send_sem=opt_ssem.at[turn],
            recv_sem=opt_rsem.at[turn],
            device_id={"half": other_half},
            device_id_type=MESH,
        )
        copy.start()
        opt_copies.append(copy)
        opt_cols[turn, rows, :] = opt_send[turn, half]

    slot_of = []
    for run in range(halves):
        places = []
        for source in range(group):
            place = jnp.int32(0)
            for j in range(group):
                spot = dest_ref[source * group + j]
                place = jnp.where(
                    lax.div(spot, group) == tile * halves + run, lax.rem(spot, group), place
                )
            places.append(place)
        for slot in range(group):
            found = jnp.int32(0)
            for source in range(group):
                found = jnp.where(places[source] == slot, source, found)
            slot_of.append(found)

    for step in order:
        for shift in range(halves):
            if step or shift:
                source = lax.rem(tile + step, tiles) * halves + lax.rem(half + shift, halves)
                pltpu.make_async_remote_copy(
                    src_ref=sar_send.at[0, 0],
                    dst_ref=arrived.at[source],
                    send_sem=sar_ssem.at[0],
                    recv_sem=sar_rsem.at[source],
                    device_id={"half": other_half},
                    device_id_type=MESH,
                ).wait_recv()
    per_patch = group // patch_dev
    for run in range(halves):
        for slot in range(group):
            at = run * quarter + (slot % per_patch) * lines
            sar_cols[slot // per_patch, at : at + lines, :] = arrived[slot_of[run * group + slot], run]

    loads[3].wait()
    for patch in range(patch_dev):
        for c in range(chunks):
            sar_rows[patch, c] = jnp.dot(
                row_v[c], sar_cols[patch], preferred_element_type=jnp.float32
            )

    lane = lax.broadcasted_iota(jnp.int32, (chunk, width), 1)
    line = lax.broadcasted_iota(jnp.int32, (chunk, width), 0)
    shared = (lane + half) == 0
    centre = (lane + line + half) == 0

    def parts(table_rows, first):
        a, c = table_rows[:chunk, :width], table_rows[:chunk, width:]
        b, d = table_rows[chunk:, :width], table_rows[chunk:, width:]
        if first:
            a = jnp.where(centre, 0.0, a)
        return a, b, c, d

    def cross_chunk(turn, patch, c):
        oa, ob, oc, od = parts(
            jnp.dot(row_v[c], opt_cols[turn], preferred_element_type=jnp.float32), c == 0
        )
        sa, sb, sc, sd = parts(sar_rows[patch, c], c == 0)
        o_re, o_im, s_re, s_im = oa + od, oc - ob, sa + sd, sc - sb
        real = o_re * s_re + o_im * s_im
        imag = o_re * s_im - o_im * s_re
        shared_real = oa * sa + ob * sb - (od * sc - oc * sd)
        shared_imag = ob * sa - oa * sb + (oc * sc + od * sd)
        real = jnp.where(shared, shared_real, real)
        imag = jnp.where(shared, shared_imag, imag)
        o_energy = jnp.sum(o_re * o_re + o_im * o_im, axis=0, keepdims=True)
        s_energy = jnp.sum(s_re * s_re + s_im * s_im, axis=0, keepdims=True)
        return real, imag, o_energy, s_energy

    weight = jnp.where(shared[:1], 1.0, 2.0)

    def pair_copy(k, src, dst, axis, to):
        return pltpu.make_async_remote_copy(
            src_ref=src,
            dst_ref=dst,
            send_sem=pair_ssem.at[k],
            recv_sem=pair_rsem.at[k],
            device_id={axis: to},
            device_id_type=MESH,
        )

    opt_copies[0].wait_recv()
    o_sum, s_sum = 0.0, 0.0
    for c in range(chunks):
        real, imag, o_energy, s_energy = cross_chunk(0, other_band, c)
        cross_send[c, :, :width] = real.astype(jnp.bfloat16)
        cross_send[c, :, width:] = imag.astype(jnp.bfloat16)
        o_sum, s_sum = o_sum + o_energy, s_sum + s_energy
    stat_send[0:1, :] = o_sum * weight
    stat_send[1:2, :] = s_sum * weight
    stat_send[2:8, :] = jnp.zeros((6, width), jnp.float32)
    cross_copy = pair_copy(0, cross_send, cross_recv, "band", other_band)
    cross_copy.start()
    stat_copy = pair_copy(1, stat_send, stat_recv, "band", other_band)
    stat_copy.start()

    opt_copies[1].wait_recv()
    o_sum, s_sum = 0.0, 0.0
    for c in range(chunks):
        real, imag, o_energy, s_energy = cross_chunk(1, band, c)
        cross_own[c, :, :width] = real
        cross_own[c, :, width:] = imag
        o_sum, s_sum = o_sum + o_energy, s_sum + s_energy

    cross_copy.wait_recv()
    for c in range(chunks):
        total = cross_own[c] + cross_recv[c].astype(jnp.float32)
        cross_all[c * chunk : (c + 1) * chunk, :] = total.astype(jnp.bfloat16)

    loads[4].wait()

    def lag_chunk(c):
        both = jnp.dot(row_v[c], cross_all[...], preferred_element_type=jnp.float32)
        lags[c, :, :width] = (both[:chunk, :width] - both[chunk:, width:]).astype(jnp.bfloat16)
        lags[c, :, width:] = (both[:chunk, width:] + both[chunk:, :width]).astype(jnp.bfloat16)

    for i in range(per_half):
        lag_chunk(other_half * per_half + i)
    lag_copy = pair_copy(2, lags.at[pl.ds(other_half * per_half, per_half)], lag_recv, "half", other_half)
    lag_copy.start()
    for i in range(per_half):
        lag_chunk(half * per_half + i)

    spots = lax.broadcasted_iota(jnp.int32, (peak_count, extent), 1)
    ranks = lax.broadcasted_iota(jnp.int32, (peak_count, extent), 0)

    def one_hot(which):
        wanted = jnp.zeros((peak_count, extent), jnp.int32)
        for j in range(peak_count):
            wanted = jnp.where(ranks == j, peaks_ref[0, which, j], wanted)
        return jnp.where(spots == wanted, 1.0, 0.0).astype(jnp.bfloat16)

    picked = jnp.dot(
        one_hot(0), lags[...].reshape(extent, 2 * width), preferred_element_type=jnp.float32
    )
    waves = lax.dot_general(
        one_hot(1), lag_v[half], (((1,), (1,)), ((), ())), preferred_element_type=jnp.float32
    )
    stat_copy.wait_recv()
    last_send[0:8, :] = stat_recv[...]
    last_send[0:1, :] = o_sum * weight + stat_recv[0:1, :]
    last_send[1:2, :] = s_sum * weight + stat_recv[1:2, :]
    last_send[8 : 8 + peak_count, :] = jnp.broadcast_to(
        jnp.sum(picked * waves, axis=1, keepdims=True), (peak_count, width)
    )
    last_copy = pair_copy(3, last_send, last_recv, "half", other_half)
    last_copy.start()

    own_lags = lags[pl.ds(half * per_half, per_half)].reshape(quarter, 2 * width)
    surface_ref[0] = jnp.dot(own_lags, lag_v[half], preferred_element_type=jnp.float32)

    last_copy.wait_recv()
    totals = last_send[...] + last_recv[...]
    pixels = extent * extent
    o_all = jnp.sum(totals[0:1, :], axis=1, keepdims=True) / (float(pixels) * bands * pixels)
    s_all = jnp.sum(totals[1:2, :], axis=1, keepdims=True) / (float(pixels) * bands * pixels)
    norm = lax.rsqrt(bands * pixels * (o_all + EPSILON) * (s_all + EPSILON)) / pixels
    peak_ref[...] = totals[8 : 8 + peak_count, :] * norm

    lag_copy.wait_recv()
    far = jnp.dot(
        lag_recv[...].reshape(quarter, 2 * width),
        lag_v[other_half],
        preferred_element_type=jnp.float32,
    )
    surface_ref[0] = (surface_ref[0] + far) * norm

    for copy in copies + opt_copies + [cross_copy, stat_copy, lag_copy, last_copy]:
        copy.wait_send()


def fused(mesh, optical, sar, destination, peaks):
    tiles, halves, bands = mesh.shape["tile"], mesh.shape["half"], mesh.shape["band"]
    patch_dev, _, quarter, extent = optical.shape
    group = tiles * halves
    lines = sar.shape[1] // group
    peak_count = peaks.shape[2]
    chunk = quarter // 2
    chunks = extent // chunk
    width = extent // 2 // halves
    sizes = (tiles, halves, bands, patch_dev, quarter, extent, lines, chunk, peak_count)
    tables = half_tables(extent, halves, chunk)
    bf, f32 = jnp.bfloat16, jnp.float32
    wide = 2 * width
    vmem = pltpu.VMEM
    dma = pltpu.SemaphoreType.DMA
    surface, peak_rows = pl.pallas_call(
        functools.partial(kernel, sizes),
        out_shape=(
            jax.ShapeDtypeStruct((1, quarter, extent), f32),
            jax.ShapeDtypeStruct((peak_count, width), f32),
        ),
        in_specs=[pl.BlockSpec(memory_space=pltpu.SMEM)] * 2
        + [pl.BlockSpec(memory_space=pl.ANY)] * 5,
        out_specs=(pl.BlockSpec(memory_space=pltpu.VMEM), pl.BlockSpec(memory_space=pltpu.VMEM)),
        scratch_shapes=[
            vmem((group, lines, extent), bf),
            vmem((patch_dev, quarter, extent), bf),
            vmem((extent, extent), bf),
            vmem((chunks, 2 * chunk, extent), bf),
            vmem((halves, wide, extent), bf),
            vmem((tiles, halves, halves, lines, wide), bf),
            vmem((group, halves, lines, wide), bf),
            vmem((patch_dev, halves, quarter, wide), bf),
            vmem((patch_dev, extent, wide), bf),
            vmem((patch_dev, extent, wide), bf),
            vmem((patch_dev, chunks, 2 * chunk, wide), f32),
            vmem((chunks, chunk, wide), bf),
            vmem((chunks, chunk, wide), bf),
            vmem((chunks, chunk, wide), f32),
            vmem((extent, wide), bf),
            vmem((8, width), f32),
            vmem((8, width), f32),
            vmem((8 + peak_count, width), f32),
            vmem((8 + peak_count, width), f32),
            vmem((chunks, chunk, wide), bf),
            vmem((chunks // halves, chunk, wide), bf),
            dma((5,)),
            dma((group,)),
            dma((group,)),
            dma((2,)),
            dma((2,)),
            dma((4,)),
            dma((4,)),
        ],
        compiler_params=pltpu.CompilerParams(
            collective_id=0, has_side_effects=True, vmem_limit_bytes=50 * 1024 * 1024
        ),
    )(
        destination,
        peaks,
        sar.reshape(group, lines, extent),
        optical.reshape(patch_dev, quarter, extent),
        *[jnp.asarray(t) for t in tables],
    )
    return surface, peak_rows[:, 0].reshape(1, peak_count)


def fits(mesh, optical, sar, peaks):
    group = mesh.shape["tile"] * mesh.shape["half"]
    patch_dev, local_bands, quarter, extent = optical.shape
    lines = sar.shape[1] // group
    return (
        mesh.shape["half"] == 2
        and mesh.shape["band"] == 2
        and patch_dev == 2
        and local_bands == 1
        and lines % 16 == 0
        and quarter % lines == 0
        and extent % 512 == 0
        and peaks.shape[0] == 1
        and peaks.shape[2] % 8 == 0
    )


def solution(mesh):
    def local(optical, sar, destination, peaks):
        if fits(mesh, optical, sar, peaks):
            return fused(mesh, optical, sar, destination, peaks)
        return generic(optical, sar, destination, peaks)

    in_specs = (
        P(("scene", "tile"), "band", "half", None),
        P("band", ("scene", "tile", "half"), None),
        P("scene"),
        P(("scene", "tile", "band"), None, None),
    )
    out_specs = (P(("scene", "tile", "band"), "half", None), P(("scene", "tile", "band"), None))
    return jax.shard_map(local, mesh=mesh, in_specs=in_specs, out_specs=out_specs, check_vma=False)
```

profile of v0, /device:TPU:0, one launch (start us, length us, event | category | flops | bytes accessed | tf_op | source)
XLA Modules:
  0.0 34.4 jit_solution(17176133243436510912)
XLA Ops:
  0.6 0.0 copy-start.5
  0.6 0.0 copy-start.6
  0.7 0.7 %copy-done.5 = s32[1,2,8]{2,1,0:T(2,128)S(1)} copy-done((s32[1,2,8]{2,1,0:T(2,128)S(1)}, s32[1,2,8]{2,1,0:T(2,128)}, u32[]{:S(2)}) %copy-start.5) | copy-done | bytes 88
  1.3 0.0 copy-done.6
  1.3 0.0 copy-start
  1.3 1.2 %copy-done = bf16[4,256,512]{2,1,0:T(8,128)(2,1)S(1)} copy-done((bf16[4,256,512]{2,1,0:T(8,128)(2,1)S(1)}, bf16[4,256,512]{2,1,0:T(8,128)(2,1)}, u32[]{:S(2)}) %copy-start) | copy-done | bytes 1048600
  2.5 0.0 copy-start.1
  2.5 1.0 %copy-done.1 = bf16[1,512,512]{2,1,0:T(8,128)(2,1)S(1)} copy-done((bf16[1,512,512]{2,1,0:T(8,128)(2,1)S(1)}, bf16[1,512,512]{2,1,0:T(8,128)(2,1)}, u32[]{:S(2)}) %copy-start.1) | copy-done | bytes 524312
  3.6 0.0 copy-start.2
  3.6 1.0 %copy-done.2 = bf16[2,1,256,512]{3,2,1,0:T(8,128)(2,1)S(1)} copy-done((bf16[2,1,256,512]{3,2,1,0:T(8,128)(2,1)S(1)}, bf16[2,1,256,512]{3,2,1,0:T(8,128)(2,1)}, u32[]{:S(2)}) %copy-start.2) | copy-done | bytes 524312
  4.6 0.0 copy-start.3
  4.6 1.0 %copy-done.3 = bf16[2,256,512]{2,1,0:T(8,128)(2,1)S(1)} copy-done((bf16[2,256,512]{2,1,0:T(8,128)(2,1)S(1)}, bf16[2,256,512]{2,1,0:T(8,128)(2,1)}, u32[]{:S(2)}) %copy-start.3) | copy-done | bytes 524312
  5.7 0.0 copy-start.4
  5.7 1.0 %copy-done.4 = bf16[512,512]{1,0:T(8,128)(2,1)S(1)} copy-done((bf16[512,512]{1,0:T(8,128)(2,1)S(1)}, bf16[512,512]{1,0:T(8,128)(2,1)}, u32[]{:S(2)}) %copy-start.4) | copy-done | bytes 524312
  6.7 26.3 %shard_map.86 = (f32[1,256,512]{2,1,0:T(8,128)S(1)}, f32[8,128]{1,0:T(8,128)S(1)}) custom-call(s32[64]{0:T(128)S(1)} %copy-done.6, s32[1,2,8]{2,1,0:T(2,128)S(1)} %copy-done.5, bf16[8,64,512]{2,1,0:T(8,128)(2,1)S(1)} %bitcast.3, bf16[2,256,512]{2,1,0:T(8,128)(2,1)S(1)} %bitcast.4, bf16[512,512]{1,0:T(8,128)(2,1)S(1)} %copy-done.4, ...), custom_call_target="tpu_custom_call" | custom-call | tf_op jit(solution)/shard_map/pallas_call | solution.py:552
  33.0 0.6 %slice_reduce_fusion = f32[8]{0:T(128)} fusion(f32[8,128]{1,0:T(8,128)S(1)} %get-tuple-element.5), kind=kLoop, calls=%fused_computation | loop fusion | bytes 64 | tf_op jit(solution)/shard_map/slice | solution.py:601
  33.6 0.8 %copy.10 = f32[1,256,512]{2,1,0:T(8,128)} copy(f32[1,256,512]{2,1,0:T(8,128)S(1)} %get-tuple-element.8) | data formatting | bytes 1048576
Async XLA Ops:
  0.6 0.7 %copy-start.5 = (s32[1,2,8]{2,1,0:T(2,128)S(1)}, s32[1,2,8]{2,1,0:T(2,128)}, u32[]{:S(2)}) copy-start(s32[1,2,8]{2,1,0:T(2,128)} %peaks_ref.1) | copy-start | bytes 196
  0.6 0.7 %copy-start.6 = (s32[64]{0:T(128)S(1)}, s32[64]{0:T(128)}, u32[]{:S(2)}) copy-start(s32[64]{0:T(128)} %dest_ref.1) | copy-start | bytes 772
  1.3 1.2 %copy-start = (bf16[4,256,512]{2,1,0:T(8,128)(2,1)S(1)}, bf16[4,256,512]{2,1,0:T(8,128)(2,1)}, u32[]{:S(2)}) copy-start(bf16[4,256,512]{2,1,0:T(8,128)(2,1)} %constant.7.clone.row_hbm) | copy-start | bytes 3145732
  2.5 1.0 %copy-start.1 = (bf16[1,512,512]{2,1,0:T(8,128)(2,1)S(1)}, bf16[1,512,512]{2,1,0:T(8,128)(2,1)}, u32[]{:S(2)}) copy-start(bf16[1,512,512]{2,1,0:T(8,128)(2,1)} %param.8) | copy-start | bytes 1572868
  3.6 1.0 %copy-start.2 = (bf16[2,1,256,512]{3,2,1,0:T(8,128)(2,1)S(1)}, bf16[2,1,256,512]{3,2,1,0:T(8,128)(2,1)}, u32[]{:S(2)}) copy-start(bf16[2,1,256,512]{3,2,1,0:T(8,128)(2,1)} %param.7) | copy-start | bytes 1572868
  4.6 1.0 %copy-start.3 = (bf16[2,256,512]{2,1,0:T(8,128)(2,1)S(1)}, bf16[2,256,512]{2,1,0:T(8,128)(2,1)}, u32[]{:S(2)}) copy-start(bf16[2,256,512]{2,1,0:T(8,128)(2,1)} %constant.8.clone.lag_hbm) | copy-start | bytes 1572868
  5.7 1.0 %copy-start.4 = (bf16[512,512]{1,0:T(8,128)(2,1)S(1)}, bf16[512,512]{1,0:T(8,128)(2,1)}, u32[]{:S(2)}) copy-start(bf16[512,512]{1,0:T(8,128)(2,1)} %constant.6.clone.col_hbm) | copy-start | bytes 1572868
where the time goes:
time: 34.8 us; the launch traced here: 34.4 us
  Pallas kernels  26.3 us (76%)
  local copies, waits for them, and re-layouts  7.47 us (21%)
  between operations  0.66 us (2%)
    pallas_call x1, Pallas kernels, fused(): pl.pallas_call(functools.partial(kernel, sizes), out_shape=(jax.ShapeDtyp...  26.3 us
    unnamed x15, local copies, waits for them, and re-layouts  6.85 us

commit v1 on v0

--- a/solution.py
+++ b/solution.py
@@ -228,8 +228,8 @@
 
 def kernel(
     sizes,
-    dest_ref,
-    peaks_ref,
+    dest_hbm,
+    peaks_hbm,
     sar_hbm,
     opt_hbm,
     col_hbm,
@@ -237,6 +237,8 @@
     lag_hbm,
     surface_ref,
     peak_ref,
+    dest_ref,
+    peaks_ref,
     sar_v,
     opt_v,
     col_v,
@@ -279,7 +281,8 @@
     loads = [
         pltpu.make_async_copy(a, b, load_sem.at[i])
         for i, (a, b) in enumerate(
-            [(sar_hbm, sar_v), (col_hbm, col_v), (opt_hbm, opt_v), (row_hbm, row_v), (lag_hbm, lag_v)]
+            [(sar_hbm, sar_v), (col_hbm, col_v), (opt_hbm, opt_v), (row_hbm, row_v), (lag_hbm, lag_v),
+             (dest_hbm, dest_ref), (peaks_hbm, peaks_ref)]
         )
     ]
     for load in loads:
@@ -300,6 +303,7 @@
                 )
     pl.semaphore_signal(barrier, inc=1, device_id={"band": other_band}, device_id_type=MESH)
 
+    loads[5].wait()
     own_runs = [lax.div(dest_ref[me * group + j], group) for j in range(group)]
 
     def block_for(run):
@@ -488,6 +492,8 @@
 
     spots = lax.broadcasted_iota(jnp.int32, (peak_count, extent), 1)
     ranks = lax.broadcasted_iota(jnp.int32, (peak_count, extent), 0)
+
+    loads[6].wait()
 
     def one_hot(which):
         wanted = jnp.zeros((peak_count, extent), jnp.int32)
@@ -555,10 +561,11 @@
             jax.ShapeDtypeStruct((1, quarter, extent), f32),
             jax.ShapeDtypeStruct((peak_count, width), f32),
         ),
-        in_specs=[pl.BlockSpec(memory_space=pltpu.SMEM)] * 2
-        + [pl.BlockSpec(memory_space=pl.ANY)] * 5,
+        in_specs=[pl.BlockSpec(memory_space=pltpu.HBM)] * 7,
         out_specs=(pl.BlockSpec(memory_space=pltpu.VMEM), pl.BlockSpec(memory_space=pltpu.VMEM)),
         scratch_shapes=[
+            pltpu.SMEM(destination.shape, jnp.int32),
+            pltpu.SMEM(peaks.shape, jnp.int32),
             vmem((group, lines, extent), bf),
             vmem((patch_dev, quarter, extent), bf),
             vmem((extent, extent), bf),
@@ -580,7 +587,7 @@
             vmem((8 + peak_count, width), f32),
             vmem((chunks, chunk, wide), bf),
             vmem((chunks // halves, chunk, wide), bf),
-            dma((5,)),
+            dma((7,)),
             dma((group,)),
             dma((group,)),
             dma((2,)),
@@ -589,7 +596,7 @@
             dma((4,)),
         ],
         compiler_params=pltpu.CompilerParams(
-            collective_id=0, has_side_effects=True, vmem_limit_bytes=50 * 1024 * 1024
+            collective_id=0, has_side_effects=True, vmem_limit_bytes=67000000
         ),
     )(
         destination,

time: 34.8 us -> 30.3 us (0.87)
  local copies, waits for them, and re-layouts: 7.47 us -> 3.18 us
    unnamed x15 -> x1, local copies, waits for them, and re-layouts: 6.85 us -> 1.87 us
    slice x1, local copies, waits for them, and re-layouts: 0.63 us -> 1.31 us  [fused(): return (surface, peak_rows[:, 0].reshape(1, peak_count))]
where the time goes in v1:
time: 30.3 us; the launch traced here: 30.1 us
  Pallas kernels  26.3 us (87%)
  local copies, waits for them, and re-layouts  3.18 us (10%)
  between operations  0.64 us (2%)
    pallas_call x1, Pallas kernels, fused(): pl.pallas_call(functools.partial(kernel, sizes), out_shape=(jax.ShapeDtyp...  26.3 us
    unnamed x1, local copies, waits for them, and re-layouts  1.87 us
    slice x1, local copies, waits for them, and re-layouts, fused(): return (surface, peak_rows[:, 0].reshape(1, peak_count))  1.31 us

profile of v1, /device:TPU:0, one launch (start us, length us, event | category | flops | bytes accessed | tf_op | source)
XLA Modules:
  0.0 30.1 jit_solution(6658912429086149156)
XLA Ops:
  0.6 26.3 %shard_map.86 = (f32[1,256,512]{2,1,0:T(8,128)}, f32[8,128]{1,0:T(8,128)}) custom-call(s32[64]{0:T(128)} %dest_hbm.1, s32[1,2,8]{2,1,0:T(2,128)} %peaks_hbm.1, bf16[8,64,512]{2,1,0:T(8,128)(2,1)} %bitcast.3, bf16[2,256,512]{2,1,0:T(8,128)(2,1)} %bitcast.4, bf16[512,512]{1,0:T(8,128)(2,1)} %constant.6.clone.col_hbm, ...), custom_call_target="tpu_custom_call" | custom-call | tf_op jit(solution)/shard_map/pallas_call | solution.py:558
  27.0 1.3 %slice_reduce_fusion = f32[8]{0:T(128)} fusion(f32[8,128]{1,0:T(8,128)} %get-tuple-element.5), kind=kLoop, calls=%fused_computation | loop fusion | bytes 64 | tf_op jit(solution)/shard_map/slice | solution.py:608
  28.3 1.9 %copy.10 = f32[1,256,512]{2,1,0:T(8,128)} copy(f32[1,256,512]{2,1,0:T(8,128)} %get-tuple-element.8) | data formatting | bytes 1048576

commit v2 on v1

--- a/solution.py
+++ b/solution.py
@@ -312,10 +312,6 @@
             found = jnp.where(own_runs[j] == run, j, found)
         return found
 
-    loads[0].wait()
-    loads[1].wait()
-    pl.semaphore_wait(barrier, group)
-
     def sar_copy(step, shift):
         to_half = lax.rem(half + shift, halves)
         return pltpu.make_async_remote_copy(
@@ -327,7 +323,8 @@
             device_id_type=MESH,
         )
 
-    copies = []
+    loads[0].wait()
+    loads[1].wait()
     order = sorted(range(tiles), key=lambda s: -min(s, tiles - s))
     for step in order:
         to_tile = lax.rem(tile + step, tiles)
@@ -339,21 +336,27 @@
         for to_half in range(halves):
             piece = spectra[:, to_half * 2 * width : (to_half + 1) * 2 * width]
             sar_send[step, to_half] = piece.reshape(halves, lines, 2 * width)
-        for shift in reversed(range(halves)):
-            if step or shift:
-                copy = sar_copy(step, shift)
-                copy.start()
-                copies.append(copy)
     arrived[me] = sar_send[0, half]
 
-    opt_copies = []
+    rows = pl.ds(pl.multiple_of(half * quarter, quarter), quarter)
     loads[2].wait()
     for turn, patch in enumerate((other_band, band)):
         spectra = jnp.dot(opt_v[patch], col_v[...], preferred_element_type=jnp.float32)
         spectra = spectra.astype(jnp.bfloat16)
         for to_half in range(halves):
             opt_send[turn, to_half] = spectra[:, to_half * 2 * width : (to_half + 1) * 2 * width]
-        rows = pl.ds(pl.multiple_of(half * quarter, quarter), quarter)
+        opt_cols[turn, rows, :] = opt_send[turn, half]
+
+    pl.semaphore_wait(barrier, group)
+    copies = []
+    for step in order:
+        for shift in reversed(range(halves)):
+            if step or shift:
+                copy = sar_copy(step, shift)
+                copy.start()
+                copies.append(copy)
+    opt_copies = []
+    for turn in range(2):
         copy = pltpu.make_async_remote_copy(
             src_ref=opt_send.at[turn, other_half],
             dst_ref=opt_cols.at[turn, rows],
@@ -364,7 +367,6 @@
         )
         copy.start()
         opt_copies.append(copy)
-        opt_cols[turn, rows, :] = opt_send[turn, half]
 
     slot_of = []
     for run in range(halves):
@@ -596,14 +598,19 @@
             dma((4,)),
         ],
         compiler_params=pltpu.CompilerParams(
-            collective_id=0, has_side_effects=True, vmem_limit_bytes=67000000
+            collective_id=0, has_side_effects=True, vmem_limit_bytes=50 * 1024 * 1024
         ),
     )(
-        destination,
-        peaks,
-        sar.reshape(group, lines, extent),
-        optical.reshape(patch_dev, quarter, extent),
-        *[jnp.asarray(t) for t in tables],
+        *[
+            pltpu.with_memory_space_constraint(x, pltpu.HBM)
+            for x in (
+                destination,
+                peaks,
+                sar.reshape(group, lines, extent),
+                optical.reshape(patch_dev, quarter, extent),
+                *[jnp.asarray(t) for t in tables],
+            )
+        ]
     )
     return surface, peak_rows[:, 0].reshape(1, peak_count)
 

time: 30.3 us -> 27.7 us (0.914)
  local copies, waits for them, and re-layouts: 3.18 us -> 1.42 us
  Pallas kernels: 26.3 us -> 25.5 us
    unnamed x1, local copies, waits for them, and re-layouts: 1.87 us -> 0.79 us
    pallas_call x1, Pallas kernels: 26.3 us -> 25.5 us  [fused(): pl.pallas_call(functools.partial(kernel, sizes), out_shape=(jax.ShapeDtyp...]
    slice x1, local copies, waits for them, and re-layouts: 1.31 us -> 0.63 us  [fused(): return (surface, peak_rows[:, 0].reshape(1, peak_count))]
where the time goes in v2:
time: 27.7 us; the launch traced here: 27.6 us
  Pallas kernels  25.5 us (92%)
  local copies, waits for them, and re-layouts  1.42 us (5%)
  between operations  0.64 us (2%)
    pallas_call x1, Pallas kernels, fused(): pl.pallas_call(functools.partial(kernel, sizes), out_shape=(jax.ShapeDtyp...  25.5 us
    unnamed x1, local copies, waits for them, and re-layouts  0.79 us
    slice x1, local copies, waits for them, and re-layouts, fused(): return (surface, peak_rows[:, 0].reshape(1, peak_count))  0.63 us

profile of v2, /device:TPU:0, one launch (start us, length us, event | category | flops | bytes accessed | tf_op | source)
XLA Modules:
  0.0 27.6 jit_solution(7585294005772244153)
XLA Ops:
  0.6 25.5 %shard_map.86 = (f32[1,256,512]{2,1,0:T(8,128)S(1)}, f32[8,128]{1,0:T(8,128)S(1)}) custom-call(s32[64]{0:T(128)} %dest_hbm.1, s32[1,2,8]{2,1,0:T(2,128)} %peaks_hbm.1, bf16[8,64,512]{2,1,0:T(8,128)(2,1)} %bitcast.3, bf16[2,256,512]{2,1,0:T(8,128)(2,1)} %bitcast.4, bf16[512,512]{1,0:T(8,128)(2,1)} %constant.6.clone.col_hbm, ...), custom_call_target="tpu_custom_call" | custom-call | tf_op jit(solution)/shard_map/pallas_call | solution.py:560
  26.2 0.6 %slice_reduce_fusion = f32[8]{0:T(128)} fusion(f32[8,128]{1,0:T(8,128)S(1)} %get-tuple-element.5), kind=kLoop, calls=%fused_computation | loop fusion | bytes 64 | tf_op jit(solution)/shard_map/slice | solution.py:615
  26.8 0.8 %copy.10 = f32[1,256,512]{2,1,0:T(8,128)} copy(f32[1,256,512]{2,1,0:T(8,128)S(1)} %get-tuple-element.8) | data formatting | bytes 1048576

commit v3 on v2

--- a/solution.py
+++ b/solution.py
@@ -236,7 +236,7 @@
     row_hbm,
     lag_hbm,
     surface_ref,
-    peak_ref,
+    total_ref,
     dest_ref,
     peaks_ref,
     sar_v,
@@ -285,8 +285,8 @@
              (dest_hbm, dest_ref), (peaks_hbm, peaks_ref)]
         )
     ]
-    for load in loads:
-        load.start()
+    for i in (5, 0, 1, 2):
+        loads[i].start()
 
     barrier = pltpu.get_barrier_semaphore()
     for step in range(tiles):
@@ -325,8 +325,10 @@
 
     loads[0].wait()
     loads[1].wait()
+    copies = []
+    opt_copies = []
     order = sorted(range(tiles), key=lambda s: -min(s, tiles - s))
-    for step in order:
+    for turn, step in enumerate(order):
         to_tile = lax.rem(tile + step, tiles)
         samples = jnp.concatenate(
             [sar_v[block_for(to_tile * halves + run)] for run in range(halves)], axis=0
@@ -336,6 +338,17 @@
         for to_half in range(halves):
             piece = spectra[:, to_half * 2 * width : (to_half + 1) * 2 * width]
             sar_send[step, to_half] = piece.reshape(halves, lines, 2 * width)
+        if turn == 0:
+            for i in (3, 4, 6):
+                loads[i].start()
+        if turn == 1:
+            pl.semaphore_wait(barrier, group)
+        for ready in order[:2] if turn == 1 else (order[turn : turn + 1] if turn > 1 else ()):
+            for shift in reversed(range(halves)):
+                if ready or shift:
+                    copy = sar_copy(ready, shift)
+                    copy.start()
+                    copies.append(copy)
     arrived[me] = sar_send[0, half]
 
     rows = pl.ds(pl.multiple_of(half * quarter, quarter), quarter)
@@ -345,18 +358,6 @@
         spectra = spectra.astype(jnp.bfloat16)
         for to_half in range(halves):
             opt_send[turn, to_half] = spectra[:, to_half * 2 * width : (to_half + 1) * 2 * width]
-        opt_cols[turn, rows, :] = opt_send[turn, half]
-
-    pl.semaphore_wait(barrier, group)
-    copies = []
-    for step in order:
-        for shift in reversed(range(halves)):
-            if step or shift:
-                copy = sar_copy(step, shift)
-                copy.start()
-                copies.append(copy)
-    opt_copies = []
-    for turn in range(2):
         copy = pltpu.make_async_remote_copy(
             src_ref=opt_send.at[turn, other_half],
             dst_ref=opt_cols.at[turn, rows],
@@ -367,6 +368,7 @@
         )
         copy.start()
         opt_copies.append(copy)
+        opt_cols[turn, rows, :] = opt_send[turn, half]
 
     slot_of = []
     for run in range(halves):
@@ -485,10 +487,13 @@
         lags[c, :, :width] = (both[:chunk, :width] - both[chunk:, width:]).astype(jnp.bfloat16)
         lags[c, :, width:] = (both[:chunk, width:] + both[chunk:, :width]).astype(jnp.bfloat16)
 
+    lag_copies = []
     for i in range(per_half):
-        lag_chunk(other_half * per_half + i)
-    lag_copy = pair_copy(2, lags.at[pl.ds(other_half * per_half, per_half)], lag_recv, "half", other_half)
-    lag_copy.start()
+        at = other_half * per_half + i
+        lag_chunk(at)
+        copy = pair_copy(3 + i, lags.at[at], lag_recv.at[i], "half", other_half)
+        copy.start()
+        lag_copies.append(copy)
     for i in range(per_half):
         lag_chunk(half * per_half + i)
 
@@ -516,30 +521,49 @@
     last_send[8 : 8 + peak_count, :] = jnp.broadcast_to(
         jnp.sum(picked * waves, axis=1, keepdims=True), (peak_count, width)
     )
-    last_copy = pair_copy(3, last_send, last_recv, "half", other_half)
+    last_copy = pair_copy(2, last_send, last_recv, "half", other_half)
     last_copy.start()
 
-    own_lags = lags[pl.ds(half * per_half, per_half)].reshape(quarter, 2 * width)
-    surface_ref[0] = jnp.dot(own_lags, lag_v[half], preferred_element_type=jnp.float32)
+    for i in range(per_half):
+        at = slice(i * chunk, (i + 1) * chunk)
+        near = lags[half * per_half + i]
+        surface_ref[0, at, :] = jnp.dot(near, lag_v[half], preferred_element_type=jnp.float32)
+
+    for i in range(per_half):
+        at = slice(i * chunk, (i + 1) * chunk)
+        lag_copies[i].wait_recv()
+        far = jnp.dot(lag_recv[i], lag_v[other_half], preferred_element_type=jnp.float32)
+        surface_ref[0, at, :] = surface_ref[0, at, :] + far
 
     last_copy.wait_recv()
-    totals = last_send[...] + last_recv[...]
+    total_ref[...] = last_send[...] + last_recv[...]
+    for copy in copies + opt_copies + lag_copies + [cross_copy, stat_copy, last_copy]:
+        copy.wait_send()
+
+
+def finish(bands, pieces, surface_ref, total_ref, out_ref, peak_ref, scaled, sem):
+    _, lines, extent = surface_ref.shape
     pixels = extent * extent
-    o_all = jnp.sum(totals[0:1, :], axis=1, keepdims=True) / (float(pixels) * bands * pixels)
-    s_all = jnp.sum(totals[1:2, :], axis=1, keepdims=True) / (float(pixels) * bands * pixels)
+    peak_count = peak_ref.shape[1]
+    width = total_ref.shape[1]
+    o_all = jnp.sum(total_ref[0:1, :], axis=1, keepdims=True) / (float(pixels) * bands * pixels)
+    s_all = jnp.sum(total_ref[1:2, :], axis=1, keepdims=True) / (float(pixels) * bands * pixels)
     norm = lax.rsqrt(bands * pixels * (o_all + EPSILON) * (s_all + EPSILON)) / pixels
-    peak_ref[...] = totals[8 : 8 + peak_count, :] * norm
-
-    lag_copy.wait_recv()
-    far = jnp.dot(
-        lag_recv[...].reshape(quarter, 2 * width),
-        lag_v[other_half],
-        preferred_element_type=jnp.float32,
-    )
-    surface_ref[0] = (surface_ref[0] + far) * norm
-
-    for copy in copies + opt_copies + [cross_copy, stat_copy, lag_copy, last_copy]:
-        copy.wait_send()
+    part = lines // pieces
+    copies = []
+    for i in range(pieces):
+        at = pl.ds(i * part, part)
+        scaled[at, :] = surface_ref[0, at, :] * norm
+        copy = pltpu.make_async_copy(scaled.at[at], out_ref.at[0, at], sem.at[i])
+        copy.start()
+        copies.append(copy)
+    values = total_ref[8 : 8 + peak_count, :] * norm
+    lane = lax.broadcasted_iota(jnp.int32, (peak_count, width), 1)
+    rank = lax.broadcasted_iota(jnp.int32, (peak_count, width), 0)
+    row = jnp.sum(jnp.where(lane == rank, values, 0.0), axis=0, keepdims=True)
+    peak_ref[...] = row[:, :peak_count]
+    for copy in copies:
+        copy.wait()
 
 
 def fused(mesh, optical, sar, destination, peaks):
@@ -557,11 +581,11 @@
     wide = 2 * width
     vmem = pltpu.VMEM
     dma = pltpu.SemaphoreType.DMA
-    surface, peak_rows = pl.pallas_call(
+    raw, totals = pl.pallas_call(
         functools.partial(kernel, sizes),
         out_shape=(
             jax.ShapeDtypeStruct((1, quarter, extent), f32),
-            jax.ShapeDtypeStruct((peak_count, width), f32),
+            jax.ShapeDtypeStruct((8 + peak_count, width), f32),
         ),
         in_specs=[pl.BlockSpec(memory_space=pltpu.HBM)] * 7,
         out_specs=(pl.BlockSpec(memory_space=pltpu.VMEM), pl.BlockSpec(memory_space=pltpu.VMEM)),
@@ -594,8 +618,8 @@
             dma((group,)),
             dma((2,)),
             dma((2,)),
-            dma((4,)),
-            dma((4,)),
+            dma((3 + chunks // halves,)),
+            dma((3 + chunks // halves,)),
         ],
         compiler_params=pltpu.CompilerParams(
             collective_id=0, has_side_effects=True, vmem_limit_bytes=50 * 1024 * 1024
@@ -612,7 +636,17 @@
             )
         ]
     )
-    return surface, peak_rows[:, 0].reshape(1, peak_count)
+    pieces = 4
+    return pl.pallas_call(
+        functools.partial(finish, bands, pieces),
+        out_shape=(
+            jax.ShapeDtypeStruct((1, quarter, extent), f32),
+            jax.ShapeDtypeStruct((1, peak_count), f32),
+        ),
+        in_specs=[pl.BlockSpec(memory_space=pltpu.VMEM)] * 2,
+        out_specs=(pl.BlockSpec(memory_space=pltpu.HBM), pl.BlockSpec(memory_space=pltpu.VMEM)),
+        scratch_shapes=[vmem((quarter, extent), f32), dma((pieces,))],
+    )(*[pltpu.with_memory_space_constraint(x, pltpu.VMEM) for x in (raw, totals)])
 
 
 def fits(mesh, optical, sar, peaks):

time: 27.7 us -> 26.9 us (0.971)
  local copies, waits for them, and re-layouts: 1.42 us -> 0 us
  Pallas kernels: 25.5 us -> 26.1 us
    pallas_call x0 -> x1, Pallas kernels: none -> 1.43 us  [fused(): pl.pallas_call(functools.partial(finish, bands, pieces), out_shape=(jax.S...]
    pallas_call x1, Pallas kernels: 25.5 us -> 24.7 us  [fused(): pl.pallas_call(functools.partial(kernel, sizes), out_shape=(jax.ShapeDtyp...]
    unnamed x1 -> x0, local copies, waits for them, and re-layouts: 0.79 us -> none
    slice x1 -> x0, local copies, waits for them, and re-layouts: 0.63 us -> none  [fused(): return (surface, peak_rows[:, 0].reshape(1, peak_count))]
where the time goes in v3:
time: 26.9 us; the launch traced here: 26.8 us
  Pallas kernels  26.1 us (97%)
  between operations  0.64 us (2%)
    pallas_call x1, Pallas kernels, fused(): pl.pallas_call(functools.partial(kernel, sizes), out_shape=(jax.ShapeDtyp...  24.7 us
    pallas_call x1, Pallas kernels, fused(): pl.pallas_call(functools.partial(finish, bands, pieces), out_shape=(jax.S...  1.43 us

profile of v3, /device:TPU:0, one launch (start us, length us, event | category | flops | bytes accessed | tf_op | source)
XLA Modules:
  0.0 26.8 jit_solution(5379853167961945702)
XLA Ops:
  0.6 24.7 %shard_map.86 = (f32[1,256,512]{2,1,0:T(8,128)S(1)}, f32[16,128]{1,0:T(8,128)S(1)}) custom-call(s32[64]{0:T(128)} %dest_hbm.1, s32[1,2,8]{2,1,0:T(2,128)} %peaks_hbm.1, bf16[8,64,512]{2,1,0:T(8,128)(2,1)} %bitcast.2, bf16[2,256,512]{2,1,0:T(8,128)(2,1)} %bitcast.3, bf16[512,512]{1,0:T(8,128)(2,1)} %constant.6.clone.col_hbm, ...), custom_call_target="tpu_custom_call" | custom-call | tf_op jit(solution)/shard_map/pallas_call | solution.py:584
  25.4 1.4 %shard_map.87 = (f32[1,256,512]{2,1,0:T(8,128)}, f32[1,8]{1,0:T(1,128)}) custom-call(f32[1,256,512]{2,1,0:T(8,128)S(1)} %get-tuple-element.4.surface_ref, f32[16,128]{1,0:T(8,128)S(1)} %get-tuple-element.5.total_ref), custom_call_target="tpu_custom_call" | custom-call | tf_op jit(solution)/shard_map/pallas_call | solution.py:640

commit v4 on v3

--- a/solution.py
+++ b/solution.py
@@ -247,12 +247,12 @@
     sar_send,
     arrived,
     opt_send,
-    opt_cols,
+    opt_far,
+    opt_near,
     sar_cols,
     sar_rows,
     cross_send,
     cross_recv,
-    cross_own,
     cross_all,
     stat_send,
     stat_recv,
@@ -351,7 +351,6 @@
                     copies.append(copy)
     arrived[me] = sar_send[0, half]
 
-    rows = pl.ds(pl.multiple_of(half * quarter, quarter), quarter)
     loads[2].wait()
     for turn, patch in enumerate((other_band, band)):
         spectra = jnp.dot(opt_v[patch], col_v[...], preferred_element_type=jnp.float32)
@@ -360,7 +359,7 @@
             opt_send[turn, to_half] = spectra[:, to_half * 2 * width : (to_half + 1) * 2 * width]
         copy = pltpu.make_async_remote_copy(
             src_ref=opt_send.at[turn, other_half],
-            dst_ref=opt_cols.at[turn, rows],
+            dst_ref=opt_far.at[turn],
             send_sem=opt_ssem.at[turn],
             recv_sem=opt_rsem.at[turn],
             device_id={"half": other_half},
@@ -368,7 +367,6 @@
         )
         copy.start()
         opt_copies.append(copy)
-        opt_cols[turn, rows, :] = opt_send[turn, half]
 
     slot_of = []
     for run in range(halves):
@@ -386,6 +384,15 @@
             for source in range(group):
                 found = jnp.where(places[source] == slot, source, found)
             slot_of.append(found)
+
+    near_lines = pl.ds(pl.multiple_of(half * quarter, quarter), quarter)
+    far_lines = pl.ds(pl.multiple_of(other_half * quarter, quarter), quarter)
+    loads[3].wait()
+    for turn in range(2):
+        for c in range(chunks):
+            opt_near[turn, c] = jnp.dot(
+                row_v[c, :, near_lines], opt_send[turn, half], preferred_element_type=jnp.float32
+            )
 
     for step in order:
         for shift in range(halves):
@@ -405,7 +412,6 @@
             at = run * quarter + (slot % per_patch) * lines
             sar_cols[slot // per_patch, at : at + lines, :] = arrived[slot_of[run * group + slot], run]
 
-    loads[3].wait()
     for patch in range(patch_dev):
         for c in range(chunks):
             sar_rows[patch, c] = jnp.dot(
@@ -425,9 +431,10 @@
         return a, b, c, d
 
     def cross_chunk(turn, patch, c):
-        oa, ob, oc, od = parts(
-            jnp.dot(row_v[c], opt_cols[turn], preferred_element_type=jnp.float32), c == 0
+        far = jnp.dot(
+            row_v[c, :, far_lines], opt_far[turn], preferred_element_type=jnp.float32
         )
+        oa, ob, oc, od = parts(opt_near[turn, c] + far, c == 0)
         sa, sb, sc, sd = parts(sar_rows[patch, c], c == 0)
         o_re, o_im, s_re, s_im = oa + od, oc - ob, sa + sd, sc - sb
         real = o_re * s_re + o_im * s_im
@@ -468,17 +475,16 @@
     stat_copy.start()
 
     opt_copies[1].wait_recv()
+    cross_copy.wait_recv()
     o_sum, s_sum = 0.0, 0.0
     for c in range(chunks):
         real, imag, o_energy, s_energy = cross_chunk(1, band, c)
-        cross_own[c, :, :width] = real
-        cross_own[c, :, width:] = imag
+        at = slice(c * chunk, (c + 1) * chunk)
+        real = real + cross_recv[c, :, :width].astype(jnp.float32)
+        imag = imag + cross_recv[c, :, width:].astype(jnp.float32)
+        cross_all[at, :width] = real.astype(jnp.bfloat16)
+        cross_all[at, width:] = imag.astype(jnp.bfloat16)
         o_sum, s_sum = o_sum + o_energy, s_sum + s_energy
-
-    cross_copy.wait_recv()
-    for c in range(chunks):
-        total = cross_own[c] + cross_recv[c].astype(jnp.float32)
-        cross_all[c * chunk : (c + 1) * chunk, :] = total.astype(jnp.bfloat16)
 
     loads[4].wait()
 
@@ -600,12 +606,12 @@
             vmem((tiles, halves, halves, lines, wide), bf),
             vmem((group, halves, lines, wide), bf),
             vmem((patch_dev, halves, quarter, wide), bf),
-            vmem((patch_dev, extent, wide), bf),
+            vmem((patch_dev, quarter, wide), bf),
+            vmem((patch_dev, chunks, 2 * chunk, wide), f32),
             vmem((patch_dev, extent, wide), bf),
             vmem((patch_dev, chunks, 2 * chunk, wide), f32),
             vmem((chunks, chunk, wide), bf),
             vmem((chunks, chunk, wide), bf),
-            vmem((chunks, chunk, wide), f32),
             vmem((extent, wide), bf),
             vmem((8, width), f32),
             vmem((8, width), f32),

time: 26.9 us -> 27.4 us (1.019)
  Pallas kernels: 26.1 us -> 26.6 us
    pallas_call x1, Pallas kernels: 24.7 us -> 25.1 us  [fused(): pl.pallas_call(functools.partial(kernel, sizes), out_shape=(jax.ShapeDtyp...]
where the time goes in v4:
time: 27.4 us; the launch traced here: 27.2 us
  Pallas kernels  26.6 us (97%)
  between operations  0.64 us (2%)
    pallas_call x1, Pallas kernels, fused(): pl.pallas_call(functools.partial(kernel, sizes), out_shape=(jax.ShapeDtyp...  25.1 us
    pallas_call x1, Pallas kernels, fused(): pl.pallas_call(functools.partial(finish, bands, pieces), out_shape=(jax.S...  1.43 us

profile of v4, /device:TPU:0, one launch (start us, length us, event | category | flops | bytes accessed | tf_op | source)
XLA Modules:
  0.0 27.2 jit_solution(10859610825195420838)
XLA Ops:
  0.6 25.1 %shard_map.86 = (f32[1,256,512]{2,1,0:T(8,128)S(1)}, f32[16,128]{1,0:T(8,128)S(1)}) custom-call(s32[64]{0:T(128)} %dest_hbm.1, s32[1,2,8]{2,1,0:T(2,128)} %peaks_hbm.1, bf16[8,64,512]{2,1,0:T(8,128)(2,1)} %bitcast.2, bf16[2,256,512]{2,1,0:T(8,128)(2,1)} %bitcast.3, bf16[512,512]{1,0:T(8,128)(2,1)} %constant.6.clone.col_hbm, ...), custom_call_target="tpu_custom_call" | custom-call | tf_op jit(solution)/shard_map/pallas_call | solution.py:590
  25.8 1.4 %shard_map.87 = (f32[1,256,512]{2,1,0:T(8,128)}, f32[1,8]{1,0:T(1,128)}) custom-call(f32[1,256,512]{2,1,0:T(8,128)S(1)} %get-tuple-element.4.surface_ref, f32[16,128]{1,0:T(8,128)S(1)} %get-tuple-element.5.total_ref), custom_call_target="tpu_custom_call" | custom-call | tf_op jit(solution)/shard_map/pallas_call | solution.py:646

commit v5 on v3

--- a/solution.py
+++ b/solution.py
@@ -252,7 +252,6 @@
     sar_rows,
     cross_send,
     cross_recv,
-    cross_own,
     cross_all,
     stat_send,
     stat_recv,
@@ -467,18 +466,17 @@
     stat_copy = pair_copy(1, stat_send, stat_recv, "band", other_band)
     stat_copy.start()
 
+    cross_copy.wait_recv()
     opt_copies[1].wait_recv()
     o_sum, s_sum = 0.0, 0.0
     for c in range(chunks):
         real, imag, o_energy, s_energy = cross_chunk(1, band, c)
-        cross_own[c, :, :width] = real
-        cross_own[c, :, width:] = imag
+        at = slice(c * chunk, (c + 1) * chunk)
+        real = real + cross_recv[c, :, :width].astype(jnp.float32)
+        imag = imag + cross_recv[c, :, width:].astype(jnp.float32)
+        cross_all[at, :width] = real.astype(jnp.bfloat16)
+        cross_all[at, width:] = imag.astype(jnp.bfloat16)
         o_sum, s_sum = o_sum + o_energy, s_sum + s_energy
-
-    cross_copy.wait_recv()
-    for c in range(chunks):
-        total = cross_own[c] + cross_recv[c].astype(jnp.float32)
-        cross_all[c * chunk : (c + 1) * chunk, :] = total.astype(jnp.bfloat16)
 
     loads[4].wait()
 
@@ -605,7 +603,6 @@
             vmem((patch_dev, chunks, 2 * chunk, wide), f32),
             vmem((chunks, chunk, wide), bf),
             vmem((chunks, chunk, wide), bf),
-            vmem((chunks, chunk, wide), f32),
             vmem((extent, wide), bf),
             vmem((8, width), f32),
             vmem((8, width), f32),
@@ -636,7 +633,7 @@
             )
         ]
     )
-    pieces = 4
+    pieces = 2
     return pl.pallas_call(
         functools.partial(finish, bands, pieces),
         out_shape=(

time: 26.9 us -> 27.5 us (1.022)
  Pallas kernels: 26.1 us -> 26.7 us
    pallas_call x1, Pallas kernels: 24.7 us -> 25.3 us  [fused(): pl.pallas_call(functools.partial(kernel, sizes), out_shape=(jax.ShapeDtyp...]
where the time goes in v5:
time: 27.5 us; the launch traced here: 27.4 us
  Pallas kernels  26.7 us (97%)
  between operations  0.64 us (2%)
    pallas_call x1, Pallas kernels, fused(): pl.pallas_call(functools.partial(kernel, sizes), out_shape=(jax.ShapeDtyp...  25.3 us
    pallas_call x1, Pallas kernels, fused(): pl.pallas_call(functools.partial(finish, bands, pieces), out_shape=(jax.S...  1.42 us

profile of v5, /device:TPU:0, one launch (start us, length us, event | category | flops | bytes accessed | tf_op | source)
XLA Modules:
  0.0 27.4 jit_solution(15149426437566782746)
XLA Ops:
  0.6 25.3 %shard_map.86 = (f32[1,256,512]{2,1,0:T(8,128)S(1)}, f32[16,128]{1,0:T(8,128)S(1)}) custom-call(s32[64]{0:T(128)} %dest_hbm.1, s32[1,2,8]{2,1,0:T(2,128)} %peaks_hbm.1, bf16[8,64,512]{2,1,0:T(8,128)(2,1)} %bitcast.2, bf16[2,256,512]{2,1,0:T(8,128)(2,1)} %bitcast.3, bf16[512,512]{1,0:T(8,128)(2,1)} %constant.6.clone.col_hbm, ...), custom_call_target="tpu_custom_call" | custom-call | tf_op jit(solution)/shard_map/pallas_call | solution.py:582
  25.9 1.4 %shard_map.87 = (f32[1,256,512]{2,1,0:T(8,128)}, f32[1,8]{1,0:T(1,128)}) custom-call(f32[1,256,512]{2,1,0:T(8,128)S(1)} %get-tuple-element.4.surface_ref, f32[16,128]{1,0:T(8,128)S(1)} %get-tuple-element.5.total_ref), custom_call_target="tpu_custom_call" | custom-call | tf_op jit(solution)/shard_map/pallas_call | solution.py:637
